TPU v7x, 512 devices: a whole 4x8x8 slice. The times are simulated.
512 devices in a mesh: fsdp: 64 (over x, y, core), dp: 8 (over z).
Axes of the slice: x: 4, y: 8, z: 8, core: 2. Of those that a mesh axis runs over, the one named last changes fastest.
Arguments:
- grads: bfloat16 [8, 1024, 28672], P('dp', 'fsdp')
- block_slot: int32 [28], replicated, may hold values from 0 to 63, as said below
- left_stats: float32 [64, 1024, 1024], P('fsdp', 'dp')
- right_stats: float32 [64, 1024, 1024], P('fsdp', 'dp')
- left_root: bfloat16 [64, 1024, 1024], P('fsdp', 'dp')
- right_root: bfloat16 [64, 1024, 1024], P('fsdp', 'dp')
Outputs:
- left_new: float32 [64, 1024, 1024], P('fsdp', 'dp')
- right_new: float32 [64, 1024, 1024], P('fsdp', 'dp')
- update: bfloat16 [1024, 28672], P('fsdp')
Inputs may be any that keep to these rules, and one draw needn't show every extreme that they name: The entries of block_slot are distinct. Block b's statistics and roots sit in slot block_slot[b], which belongs to the fsdp device of index block_slot[b]; slots that no block names are empty and their statistics pass through unchanged.
All inputs are finite; a program needn't handle non-finite values.
Results may differ from a plain program's by a relative error of at most 0.015.
Values may be sent and summed in bfloat16 or wider, within the bound.
No kernel may reach another device: no remote copies, remote signals or barrier semaphores. Data moves between devices by JAX's collectives and lax.ppermute only.
A program may use at most 64 MiB of HBM per device.

v0:
```python
import jax
import jax.numpy as jnp
from jax import lax
from jax.sharding import Mesh
from jax.sharding import PartitionSpec as P

FSDP = ("fsdp_0", "fsdp_1", "fsdp_2")
epsilon = 1e-06


def in_blocks(array, dim, count):
    lengths = array.shape
    tiles = array.reshape(*lengths[:dim], count, lengths[dim] // count, *lengths[dim + 1 :])
    return jnp.moveaxis(tiles, dim, 0)


def sum_at_owner(array, axis, dim):
    count = lax.axis_size(axis)
    tiles = lax.all_to_all(in_blocks(array, dim, count), axis, 0, 0, tiled=True)
    return jnp.sum(tiles.astype(jnp.float32), axis=0)


def in_order(tiles, dim):
    tiles = jnp.moveaxis(tiles, 0, dim)
    lengths = tiles.shape
    return tiles.reshape(*lengths[:dim], lengths[dim] * lengths[dim + 1], *lengths[dim + 2 :])


def exchange_in_order(tiles, axes, sequence):
    inside = tiles.shape[1:]
    result = tiles.reshape(*(lax.axis_size(a) for a in axes), *inside)
    for k in sequence:
        result = lax.all_to_all(result, axes[k], k, k, tiled=True)
    return result.reshape(-1, *inside)


def core_and_chips(array, groups, sequence, split_dim, concat_dim):
    count = lax.axis_size(groups[0]) * lax.axis_size(groups[1])
    tiles = in_blocks(array, split_dim, count)
    return in_order(exchange_in_order(tiles, groups, sequence), concat_dim)


def per_device(grads, block_slot, left_stats, right_stats, left_root, right_root):
    local_rows = grads[0]
    row_dev, col_count = local_rows.shape
    block_size = left_stats.shape[2]
    block_count = col_count // block_size
    slot_count = left_stats.shape[0]
    shared_rows = left_stats.shape[1]
    total_slots = slot_count * lax.axis_size(FSDP)
    slot_ids = jnp.arange(total_slots, dtype=jnp.int32)
    matches = block_slot[None, :] == slot_ids[:, None]
    filled = jnp.any(matches, axis=1)
    source = jnp.sum(
        jnp.where(matches, jnp.arange(block_count, dtype=jnp.int32)[None, :], 0), axis=1
    )
    row_start = lax.axis_index("dp") * shared_rows
    band = local_rows.astype(jnp.float32).reshape(row_dev, block_count, block_size)
    shares = sum_at_owner(band.astype(jnp.bfloat16), "dp", 2).astype(jnp.bfloat16)
    outgoing = jnp.where(
        filled[None, :, None], jnp.take(shares, source, axis=1), jnp.zeros((), jnp.bfloat16)
    )
    incoming = lax.all_to_all(outgoing, FSDP, split_axis=1, concat_axis=0, tiled=True)
    gradient = lax.all_gather(incoming, "dp", axis=2, tiled=True)
    own_rows = lax.dynamic_slice_in_dim(gradient, row_start, shared_rows, 0)
    whole_right = lax.all_gather(right_root, "dp", axis=1, tiled=True)
    left_new = left_stats + jnp.einsum(
        "rjc,kjc->jrk", own_rows, gradient, preferred_element_type=jnp.float32
    )
    columns = lax.dynamic_slice_in_dim(gradient, row_start, shared_rows, 2)
    right_new = right_stats + jnp.einsum(
        "rjc,rjk->jck", columns, gradient, preferred_element_type=jnp.float32
    )
    left_applied = jnp.einsum(
        "jrk,kjc->rjc", left_root, gradient, preferred_element_type=jnp.float32
    ).astype(jnp.bfloat16)
    both_applied = jnp.einsum(
        "rjc,jck->rjk", left_applied, whole_right, preferred_element_type=jnp.float32
    )
    squares = lax.psum(jnp.sum(both_applied * both_applied, axis=(0, 2)), "dp")
    factor = lax.rsqrt(squares / (block_size * block_size) + epsilon)
    scaled = (both_applied * factor[None, :, None]).astype(jnp.bfloat16)
    full_rows = lax.all_gather(scaled, "dp", axis=0, tiled=True)
    returned = core_and_chips(full_rows, (("fsdp_0", "fsdp_1"), "fsdp_2"), (1, 0), 0, 1)
    update = jnp.take(returned, block_slot, axis=1).reshape(row_dev, col_count)
    return (left_new, right_new, update)


def solution(mesh):
    split = Mesh(
        mesh.devices.reshape(4, 8, 2, mesh.shape["dp"]), ("fsdp_0", "fsdp_1", "fsdp_2", "dp")
    )
    placed = (
        P("dp", FSDP, None),
        P(),
        P(FSDP, "dp", None),
        P(FSDP, "dp", None),
        P(FSDP, "dp", None),
        P(FSDP, "dp", None),
    )
    return jax.shard_map(
        per_device,
        mesh=split,
        in_specs=placed,
        out_specs=(P(FSDP, "dp", None), P(FSDP, "dp", None), P(FSDP, None)),
        check_vma=False,
    )
```

profile of v0, /device:TPU:16, one launch (start us, length us, event | category | flops | bytes accessed | tf_op | source)
XLA Modules:
  0.0 264.3 jit_solution(12434636869901836517)
XLA Ops:
  7.2 0.0 copy-start
  7.2 0.0 all-gather.6.cloned.1.call-start
  7.2 0.7 all-gather.6.cloned.1.call-update
  7.9 1.3 copy.35
  9.2 0.0 copy-start.4
  9.2 1.3 copy.27
  10.5 10.3 %all-to-all-start = ((bf16[8,16,28,128]{3,1,2,0:T(8,128)(2,1)}), bf16[8,16,28,128]{3,1,2,0:T(8,128)(2,1)S(1)}, u32[]{:S(2)}, u32[]{:S(2)}) async-start(bf16[8,16,28,128]{3,1,2,0:T(8,128)(2,1)} %copy.27), calls=%async_computation | async-start | bytes 1835008 | tf_op jit(solution)/shard_map/all_to_all | solution.py:19
  20.8 0.0 all-gather.4.cloned.1.call-start
  20.9 0.0 copy-done.4
  20.9 0.1 select_reduce_fusion
  21.0 0.1 fusion.35
  21.1 32.4 %all-to-all-done = bf16[8,16,28,128]{3,1,2,0:T(8,128)(2,1)S(1)} async-done(((bf16[8,16,28,128]{3,1,2,0:T(8,128)(2,1)}), bf16[8,16,28,128]{3,1,2,0:T(8,128)(2,1)S(1)}, u32[]{:S(2)}, u32[]{:S(2)}) %all-to-all-start) | async-done | bytes 917536 | tf_op jit(solution)/shard_map/all_to_all | solution.py:19
  53.5 0.1 reduce_sum.35
  53.6 0.6 gather_fusion
  54.2 0.2 select_bitcast_fusion
  54.4 22.2 %all_to_all.33 = bf16[16,64,128]{2,0,1:T(8,128)(2,1)} all-to-all(bf16[16,64,128]{2,0,1:T(8,128)(2,1)S(1)} %select_bitcast_fusion), channel_id=1, replica_groups=mesh['fsdp_0'=4,'fsdp_1'=8,'fsdp_2'=2,'dp'=8] {'fsdp_0','fsdp_1','fsdp_2'}, dimensions={1} | all-to-all | bytes 524288 | tf_op jit(solution)/shard_map/all_to_all | solution.py:63
  76.6 0.0 all-gather.4.cloned.1.call-update
  76.6 0.0 all-gather.8.cloned.1.call-start
  76.7 0.0 all-gather.6.cloned.1.call-done
  76.7 43.8 %all-gather.4.cloned.1.call-done = bf16[1024,1,1024]{2,0,1:T(8,128)(2,1)} async-done(((bf16[1024,1,128]{2,0,1:T(8,128)(2,1)}), bf16[1024,1,1024]{2,0,1:T(8,128)(2,1)}) %all-gather.4.cloned.1.call-update) | async-done | bytes 2097168 | tf_op jit(solution)/shard_map/all_gather | solution.py:64
  120.5 0.0 copy-done
  120.5 4.3 %multiply_reduce_fusion = (f32[]{:T(128)}, f32[128,1024]{1,0:T(8,128)S(1)}) fusion(bf16[1,1024,1024]{2,1,0:T(8,128)(2,1)} %all-gather.6.cloned.1.call-done, bf16[1024,1,1024]{2,0,1:T(8,128)(2,1)} %all-gather.4.cloned.1.call-done, bf16[1,128,1024]{2,1,0:T(8,128)(2,1)S(1)} %copy-done), kind=kOutput, calls=%fused_computation.18 | convolution fusion | flops 537264128 | bytes 4980740 | tf_op jit(solution)/shard_map/rjc,jck->rjk/dot_general | solution.py:77
  124.8 17.1 %psum.7 = f32[1]{0:T(128)} all-reduce(f32[1]{0:T(128)} %bitcast.17), channel_id=1, replica_groups=mesh['fsdp_0'=4,'fsdp_1'=8,'fsdp_2'=2,'dp'=8] {'dp'}, use_global_device_ids=true, to_apply=%region_4.5 | all-reduce | flops 1 | bytes 8 | tf_op jit(solution)/shard_map/psum | solution.py:80
  142.6 0.7 fusion.28
  143.3 0.0 all-gather.8.cloned.1.call-update
  143.4 41.8 %all-gather.8.cloned.1.call-done = bf16[1024,1,1024]{2,0,1:T(8,128)(2,1)} async-done(((bf16[128,1,1024]{2,0,1:T(8,128)(2,1)}), bf16[1024,1,1024]{2,0,1:T(8,128)(2,1)}) %all-gather.8.cloned.1.call-update) | async-done | bytes 2097168 | tf_op jit(solution)/shard_map/all_gather | solution.py:83
  185.1 1.8 copy.30
  186.9 5.4 %all_to_all.34 = bf16[32,2,16,1,1024]{4,2,0,3,1:T(8,128)(2,1)S(1)} all-to-all(bf16[32,2,16,1,1024]{4,2,0,3,1:T(8,128)(2,1)S(1)} %copy.30), channel_id=1, replica_groups=mesh['fsdp_0'=4,'fsdp_1'=8,'fsdp_2'=2,'dp'=8] {'fsdp_2'}, dimensions={1} | all-to-all | bytes 4194304 | tf_op jit(solution)/shard_map/all_to_all | solution.py:33
  192.3 1.5 copy.31
  193.8 0.0 copy-start.1
  193.8 0.0 copy-start.2
  193.8 10.1 %all-to-all-start.3 = ((bf16[32,2,16,1,1024]{4,2,1,3,0:T(8,128)(2,1)}), bf16[32,2,16,1,1024]{4,2,1,3,0:T(8,128)(2,1)}, u32[]{:S(2)}, u32[]{:S(2)}) async-start(bf16[32,2,16,1,1024]{4,2,1,3,0:T(8,128)(2,1)} %copy.31), calls=%async_computation.3 | async-start | bytes 4194304 | tf_op jit(solution)/shard_map/all_to_all | solution.py:33
  204.0 0.0 copy-start.3
  204.0 0.1 broadcast_in_dim.61
  204.1 0.1 broadcast_in_dim.62
  204.2 0.0 copy-done.1
  204.2 0.0 copy-done.2
  204.2 1.3 fusion.14
  205.5 0.0 copy-done.3
  205.5 1.6 fusion.17
  207.1 47.3 %all-to-all-done.3 = bf16[32,2,16,1,1024]{4,2,1,3,0:T(8,128)(2,1)} async-done(((bf16[32,2,16,1,1024]{4,2,1,3,0:T(8,128)(2,1)}), bf16[32,2,16,1,1024]{4,2,1,3,0:T(8,128)(2,1)}, u32[]{:S(2)}, u32[]{:S(2)}) %all-to-all-start.3) | async-done | bytes 2097184 | tf_op jit(solution)/shard_map/all_to_all | solution.py:33
  254.4 2.2 gather_fusion.1
  256.6 0.1 copy.34
  256.6 1.1 broadcast_select_fusion
  (6 shorter events, 0.0 us)
Async XLA Ops:
  7.2 113.3 %copy-start = (bf16[1,128,1024]{2,1,0:T(8,128)(2,1)S(1)}, bf16[1,128,1024]{2,1,0:T(8,128)(2,1)}, u32[]{:S(2)}) copy-start(bf16[1,128,1024]{2,1,0:T(8,128)(2,1)} %param.10) | copy-start | bytes 786436
  7.2 69.5 %all-gather.6.cloned.1.call-start = ((), (), s32[]{:S(2)}) async-start(), calls=%async_computation.5 | async-start | bytes 2359296 | tf_op jit(solution)/shard_map/all_gather | solution.py:66
  9.2 11.7 %copy-start.4 = (s32[28]{0:T(128)S(1)}, s32[28]{0:T(128)}, u32[]{:S(2)}) copy-start(s32[28]{0:T(128)} %param.7) | copy-start | bytes 340
  10.5 43.0 %all-to-all-start = ((bf16[8,16,28,128]{3,1,2,0:T(8,128)(2,1)}), bf16[8,16,28,128]{3,1,2,0:T(8,128)(2,1)S(1)}, u32[]{:S(2)}, u32[]{:S(2)}) async-start(bf16[8,16,28,128]{3,1,2,0:T(8,128)(2,1)} %copy.27), calls=%async_computation | async-start | bytes 1835008 | tf_op jit(solution)/shard_map/all_to_all | solution.py:19
  20.8 99.7 %all-gather.4.cloned.1.call-start = ((), (), s32[]{:S(2)}) async-start(), calls=%async_computation.4 | async-start | bytes 2359296 | tf_op jit(solution)/shard_map/all_gather | solution.py:64
  76.6 108.5 %all-gather.8.cloned.1.call-start = ((), (), s32[]{:S(2)}) async-start(), calls=%async_computation.6 | async-start | bytes 2359296 | tf_op jit(solution)/shard_map/all_gather | solution.py:83
  193.8 10.4 %copy-start.1 = (bf16[1024,1,1024]{2,0,1:T(8,128)(2,1)S(1)}, bf16[1024,1,1024]{2,0,1:T(8,128)(2,1)}, u32[]{:S(2)}) copy-start(bf16[1024,1,1024]{2,0,1:T(8,128)(2,1)} %all-gather.4.cloned.1.call-done) | copy-start | bytes 6291460
  193.8 10.4 %copy-start.2 = (f32[1,128,1024]{2,1,0:T(8,128)S(1)}, f32[1,128,1024]{2,1,0:T(8,128)}, u32[]{:S(2)}) copy-start(f32[1,128,1024]{2,1,0:T(8,128)} %param.9) | copy-start | bytes 1572868
  193.8 60.5 %all-to-all-start.3 = ((bf16[32,2,16,1,1024]{4,2,1,3,0:T(8,128)(2,1)}), bf16[32,2,16,1,1024]{4,2,1,3,0:T(8,128)(2,1)}, u32[]{:S(2)}, u32[]{:S(2)}) async-start(bf16[32,2,16,1,1024]{4,2,1,3,0:T(8,128)(2,1)} %copy.31), calls=%async_computation.3 | async-start | bytes 4194304 | tf_op jit(solution)/shard_map/all_to_all | solution.py:33
  204.0 1.5 copy-start.3
Sparse Core Ops, SparseCore 0:
  10.1 58.1 all-gather.5
  76.8 43.6 all-gather.3
  143.5 41.6 all-gather.7
where the time goes:
time: 265 us; the launch traced here: 264 us
  waiting for transfers between devices  166 us (63%)
  blocking collectives  44.7 us (17%)
  starting transfers between devices  20.6 us (8%)
  between operations  14.6 us (6%)
  local copies, waits for them, and re-layouts  8.89 us (3%)
  matrix products  7.23 us (3%)
    all_to_all x1, waiting for transfers between devices, exchange_in_order(): result = lax.all_to_all(result, axes[k], k, k, tiled=True)  47.3 us
    all_gather x1, waiting for transfers between devices, per_device(): gradient = lax.all_gather(incoming, 'dp', axis=2, tiled=True)  43.8 us
    all_gather x1, waiting for transfers between devices, per_device(): full_rows = lax.all_gather(scaled, 'dp', axis=0, tiled=True)  41.8 us
    all_to_all x1, waiting for transfers between devices, sum_at_owner(): tiles = lax.all_to_all(in_blocks(array, dim, count), axis, 0, 0, tiled=True)  32.4 us
    all_to_all x1, blocking collectives, per_device(): lax.all_to_all(outgoing, FSDP, split_axis=1, concat_axis=0, tiled=True)  22.2 us
    psum x1, blocking collectives, per_device(): squares = lax.psum(jnp.sum(both_applied * both_applied, axis=(0, 2)), 'dp')  17.1 us
    all_to_all x1, starting transfers between devices, sum_at_owner(): tiles = lax.all_to_all(in_blocks(array, dim, count), axis, 0, 0, tiled=True)  10.3 us
    all_to_all x1, starting transfers between devices, exchange_in_order(): result = lax.all_to_all(result, axes[k], k, k, tiled=True)  10.1 us
  transfers between devices with their start and end apart: 5, of which 4 were waited for; matrix products, arithmetic and copies ran while one was open for 3% of the time, Pallas kernels for 0%

commit v1 on v0

--- a/solution.py
+++ b/solution.py
@@ -6,6 +6,12 @@
 
 FSDP = ("fsdp_0", "fsdp_1", "fsdp_2")
 epsilon = 1e-06
+
+
+def laid_out(blocks, dim):
+    blocks = jnp.moveaxis(blocks, 0, dim)
+    lengths = blocks.shape
+    return blocks.reshape(*lengths[:dim], lengths[dim] * lengths[dim + 1], *lengths[dim + 2 :])
 
 
 def in_blocks(array, dim, count):
@@ -61,7 +67,19 @@
         filled[None, :, None], jnp.take(shares, source, axis=1), jnp.zeros((), jnp.bfloat16)
     )
     incoming = lax.all_to_all(outgoing, FSDP, split_axis=1, concat_axis=0, tiled=True)
-    gradient = lax.all_gather(incoming, "dp", axis=2, tiled=True)
+    peers = lax.axis_size("dp")
+    pairs = [(i, (i + 1) % peers) for i in range(peers)]
+    back = [(b, a_2) for a_2, b in pairs]
+    lower, upper = ([], [])
+    for hop in range(peers - 1):
+        if hop % 2 == 0:
+            lower.append(lax.ppermute(lower[-1] if lower else incoming, "dp", pairs))
+        else:
+            upper.append(lax.ppermute(upper[-1] if upper else incoming, "dp", back))
+    blocks = jnp.stack([*lower[::-1], incoming, *upper])
+    shift = lax.axis_index("dp") - len(lower)
+    blocks = blocks[(jnp.arange(peers) - shift) % peers]
+    gradient = laid_out(blocks, 2)
     own_rows = lax.dynamic_slice_in_dim(gradient, row_start, shared_rows, 0)
     whole_right = lax.all_gather(right_root, "dp", axis=1, tiled=True)
     left_new = left_stats + jnp.einsum(

time: 265 us -> 258 us (0.974)
  waiting for transfers between devices: 166 us -> 125 us
  starting transfers between devices: 20.6 us -> 47 us
  local copies, waits for them, and re-layouts: 8.89 us -> 17 us
    all_gather x1 -> x0, waiting for transfers between devices: 43.8 us -> none  [per_device(): gradient = lax.all_gather(incoming, 'dp', axis=2, tiled=True)]
    ppermute x0 -> x7, starting transfers between devices: none -> 26.6 us  [the longest x4 14.6 us: per_device(): lower.append(lax.ppermute(lower[-1] if lower else incoming, 'dp', pairs))]
    ppermute x0 -> x7, waiting for transfers between devices: none -> 14.6 us  [the longest x4 14.6 us: per_device(): lower.append(lax.ppermute(lower[-1] if lower else incoming, 'dp', pairs))]
    all_to_all x1, waiting for transfers between devices: 32.4 us -> 24.4 us  [sum_at_owner(): tiles = lax.all_to_all(in_blocks(array, dim, count), axis, 0, 0, tiled=True)]
    all_gather x1, waiting for transfers between devices: 41.8 us -> 37.9 us  [per_device(): full_rows = lax.all_gather(scaled, 'dp', axis=0, tiled=True)]
    unnamed x11 -> x18, local copies, waits for them, and re-layouts: 1.33 us -> 4.46 us
    transpose x0 -> x1, local copies, waits for them, and re-layouts: none -> 2.85 us  [laid_out(): blocks = jnp.moveaxis(blocks, 0, dim)]
  transfers between devices with their start and end apart: 5 -> 11, of which waited for: 4 -> 7; matrix products, arithmetic and copies ran while one was open for 3% -> 5% of each run, Pallas kernels for 0% -> 0%
where the time goes in v1:
time: 258 us; the launch traced here: 257 us
  waiting for transfers between devices  125 us (48%)
  starting transfers between devices  47 us (18%)
  blocking collectives  44 us (17%)
  local copies, waits for them, and re-layouts  17 us (7%)
  between operations  15 us (6%)
  matrix products  6.57 us (3%)
    all_to_all x1, waiting for transfers between devices, exchange_in_order(): result = lax.all_to_all(result, axes[k], k, k, tiled=True)  47.3 us
    all_gather x1, waiting for transfers between devices, per_device(): full_rows = lax.all_gather(scaled, 'dp', axis=0, tiled=True)  37.9 us
    all_to_all x1, waiting for transfers between devices, sum_at_owner(): tiles = lax.all_to_all(in_blocks(array, dim, count), axis, 0, 0, tiled=True)  24.4 us
    all_to_all x1, blocking collectives, per_device(): lax.all_to_all(outgoing, FSDP, split_axis=1, concat_axis=0, tiled=True)  21.6 us
    psum x1, blocking collectives, per_device(): squares = lax.psum(jnp.sum(both_applied * both_applied, axis=(0, 2)), 'dp')  16.9 us
    ppermute x4, starting transfers between devices, per_device(): lower.append(lax.ppermute(lower[-1] if lower else incoming, 'dp', pairs))  14.6 us
    ppermute x4, waiting for transfers between devices, per_device(): lower.append(lax.ppermute(lower[-1] if lower else incoming, 'dp', pairs))  14.6 us
    ppermute x3, starting transfers between devices, per_device(): upper.append(lax.ppermute(upper[-1] if upper else incoming, 'dp', back))  12 us
  transfers between devices with their start and end apart: 11, of which 7 were waited for; matrix products, arithmetic and copies ran while one was open for 5% of the time, Pallas kernels for 0%

profile of v1, /device:TPU:16, one launch (start us, length us, event | category | flops | bytes accessed | tf_op | source)
XLA Modules:
  0.0 256.9 jit_solution(9030065843454904279)
XLA Ops:
  7.2 0.0 copy-start
  7.2 1.3 copy.93
  8.5 0.0 copy-start.4
  8.5 1.3 copy.74
  9.8 10.3 %all-to-all-start = ((bf16[8,16,28,128]{3,1,2,0:T(8,128)(2,1)}), bf16[8,16,28,128]{3,1,2,0:T(8,128)(2,1)S(1)}, u32[]{:S(2)}, u32[]{:S(2)}) async-start(bf16[8,16,28,128]{3,1,2,0:T(8,128)(2,1)} %copy.74), calls=%async_computation | async-start | bytes 1835008 | tf_op jit(solution)/shard_map/all_to_all | solution.py:25
  20.1 0.0 all-gather.3.cloned.1.call-start
  20.2 0.7 all-gather.3.cloned.1.call-update
  20.9 0.0 all-gather.5.cloned.1.call-start
  20.9 0.0 copy-done.4
  20.9 0.1 select_reduce_fusion
  21.0 0.1 fusion.12
  21.1 24.4 %all-to-all-done = bf16[8,16,28,128]{3,1,2,0:T(8,128)(2,1)S(1)} async-done(((bf16[8,16,28,128]{3,1,2,0:T(8,128)(2,1)}), bf16[8,16,28,128]{3,1,2,0:T(8,128)(2,1)S(1)}, u32[]{:S(2)}, u32[]{:S(2)}) %all-to-all-start) | async-done | bytes 917536 | tf_op jit(solution)/shard_map/all_to_all | solution.py:25
  45.5 0.1 reduce_sum.35
  45.7 0.6 gather_fusion
  46.3 0.2 select_bitcast_fusion
  46.5 21.6 %all_to_all.33 = bf16[16,64,128]{2,0,1:T(8,128)(2,1)S(1)} all-to-all(bf16[16,64,128]{2,0,1:T(8,128)(2,1)S(1)} %select_bitcast_fusion), channel_id=1, replica_groups=mesh['fsdp_0'=4,'fsdp_1'=8,'fsdp_2'=2,'dp'=8] {'fsdp_0','fsdp_1','fsdp_2'}, dimensions={1} | all-to-all | bytes 524288 | tf_op jit(solution)/shard_map/all_to_all | solution.py:69
  68.1 5.4 %collective-permute-start = (bf16[1024,1,128]{2,0,1:T(8,128)(2,1)S(1)}, bf16[1024,1,128]{2,0,1:T(8,128)(2,1)S(1)}, u32[]{:S(2)}, u32[]{:S(2)}) collective-permute-start(bf16[1024,1,128]{2,0,1:T(8,128)(2,1)S(1)} %bitcast.123), channel_id=1, source_target_pairs={{0,1},{1,2},{2,3},{3,4},{4,5},{5,6},{6,7},{7,0},{8,9},{9,10},{10,1... | collective-permute-start | bytes 786440 | tf_op jit(solution)/shard_map/ppermute | solution.py:76
  73.6 6.0 %collective-permute-done = bf16[1024,1,128]{2,0,1:T(8,128)(2,1)S(1)} collective-permute-done((bf16[1024,1,128]{2,0,1:T(8,128)(2,1)S(1)}, bf16[1024,1,128]{2,0,1:T(8,128)(2,1)S(1)}, u32[]{:S(2)}, u32[]{:S(2)}) %collective-permute-start) | collective-permute-done | bytes 262176 | tf_op jit(solution)/shard_map/ppermute | solution.py:76
  79.5 4.2 %collective-permute-start.1 = (bf16[1024,1,128]{2,0,1:T(8,128)(2,1)S(1)}, bf16[1024,1,128]{2,0,1:T(8,128)(2,1)S(1)}, u32[]{:S(2)}, u32[]{:S(2)}) collective-permute-start(bf16[1024,1,128]{2,0,1:T(8,128)(2,1)S(1)} %collective-permute-done), channel_id=1, source_target_pairs={{0,1},{1,2},{2,3},{3,4},{4,5},{5,6},{6,7},{7,0},{8,9},{9,10},{10,1... | collective-permute-start | bytes 786440 | tf_op jit(solution)/shard_map/ppermute | solution.py:76
  83.8 2.8 %collective-permute-start.4 = (bf16[1024,1,128]{2,0,1:T(8,128)(2,1)S(1)}, bf16[1024,1,128]{2,0,1:T(8,128)(2,1)S(1)}, u32[]{:S(2)}, u32[]{:S(2)}) collective-permute-start(bf16[1024,1,128]{2,0,1:T(8,128)(2,1)S(1)} %bitcast.124), channel_id=1, source_target_pairs={{1,0},{2,1},{3,2},{4,3},{5,4},{6,5},{7,6},{0,7},{9,8},{10,9},{11,1... | collective-permute-start | bytes 786440 | tf_op jit(solution)/shard_map/ppermute | solution.py:78
  86.6 3.5 %collective-permute-done.1 = bf16[1024,1,128]{2,0,1:T(8,128)(2,1)S(1)} collective-permute-done((bf16[1024,1,128]{2,0,1:T(8,128)(2,1)S(1)}, bf16[1024,1,128]{2,0,1:T(8,128)(2,1)S(1)}, u32[]{:S(2)}, u32[]{:S(2)}) %collective-permute-start.1) | collective-permute-done | bytes 262176 | tf_op jit(solution)/shard_map/ppermute | solution.py:76
  90.1 3.0 %collective-permute-start.2 = (bf16[1024,1,128]{2,0,1:T(8,128)(2,1)S(1)}, bf16[1024,1,128]{2,0,1:T(8,128)(2,1)S(1)}, u32[]{:S(2)}, u32[]{:S(2)}) collective-permute-start(bf16[1024,1,128]{2,0,1:T(8,128)(2,1)S(1)} %collective-permute-done.1), channel_id=1, source_target_pairs={{0,1},{1,2},{2,3},{3,4},{4,5},{5,6},{6,7},{7,0},{8,9},{9,10},{10,1... | collective-permute-start | bytes 786440 | tf_op jit(solution)/shard_map/ppermute | solution.py:76
  93.1 0.0 collective-permute-done.4
  93.1 4.0 %collective-permute-start.5 = (bf16[1024,1,128]{2,0,1:T(8,128)(2,1)S(1)}, bf16[1024,1,128]{2,0,1:T(8,128)(2,1)}, u32[]{:S(2)}, u32[]{:S(2)}) collective-permute-start(bf16[1024,1,128]{2,0,1:T(8,128)(2,1)S(1)} %collective-permute-done.4), channel_id=1, source_target_pairs={{1,0},{2,1},{3,2},{4,3},{5,4},{6,5},{7,6},{0,7},{9,8},{10,9},{11,1... | collective-permute-start | bytes 786440 | tf_op jit(solution)/shard_map/ppermute | solution.py:78
  97.2 2.6 %collective-permute-done.2 = bf16[1024,1,128]{2,0,1:T(8,128)(2,1)S(1)} collective-permute-done((bf16[1024,1,128]{2,0,1:T(8,128)(2,1)S(1)}, bf16[1024,1,128]{2,0,1:T(8,128)(2,1)S(1)}, u32[]{:S(2)}, u32[]{:S(2)}) %collective-permute-start.2) | collective-permute-done | bytes 262176 | tf_op jit(solution)/shard_map/ppermute | solution.py:76
  99.8 0.0 copy-start.3
  99.8 1.9 collective-permute-start.3
  101.8 0.0 collective-permute-done.5
  101.8 5.1 %collective-permute-start.6 = (bf16[1024,1,128]{2,0,1:T(8,128)(2,1)}, bf16[1024,1,128]{2,0,1:T(8,128)(2,1)S(1)}, u32[]{:S(2)}, u32[]{:S(2)}) collective-permute-start(bf16[1024,1,128]{2,0,1:T(8,128)(2,1)} %collective-permute-done.5), channel_id=1, source_target_pairs={{1,0},{2,1},{3,2},{4,3},{5,4},{6,5},{7,6},{0,7},{9,8},{10,9},{11,1... | collective-permute-start | bytes 786440 | tf_op jit(solution)/shard_map/ppermute | solution.py:78
  106.9 0.0 copy-done.3
  106.9 2.5 collective-permute-done.3
  109.4 1.0 bitcast_dynamic-update-slice_fusion.5
  110.4 1.0 bitcast_dynamic-update-slice_fusion.4
  111.5 1.0 bitcast_dynamic-update-slice_fusion
  112.5 0.0 collective-permute-done.6
  112.6 2.1 gather_fusion.1
  114.7 2.9 %copy.84 = bf16[1024,1,8,128]{0,3,2,1:T(8,128)(2,1)S(1)} copy(bf16[1024,1,8,128]{3,0,2,1:T(8,128)(2,1)} %bitcast.117) | data formatting | bytes 4194304 | tf_op jit(solution)/shard_map/transpose | solution.py:12
  117.5 0.0 all-gather.3.cloned.1.call-done
  117.6 0.0 copy-done
  117.6 3.7 %multiply_reduce_fusion = (f32[]{:T(128)}, f32[128,1024]{1,0:T(8,128)S(1)}) fusion(bf16[1,1024,1024]{2,1,0:T(8,128)(2,1)} %all-gather.3.cloned.1.call-done, bf16[1024,1024]{0,1:T(8,128)(2,1)S(1)} %bitcast.112, bf16[1,128,1024]{2,1,0:T(8,128)(2,1)S(1)} %copy-done), kind=kOutput, calls=%fused_computation.13 | convolution fusion | flops 537264128 | bytes 4980740 | tf_op jit(solution)/shard_map/rjc,jck->rjk/dot_general | solution.py:95
  121.2 16.9 %psum.7 = f32[1]{0:T(128)} all-reduce(f32[1]{0:T(128)} %bitcast.40), channel_id=1, replica_groups=mesh['fsdp_0'=4,'fsdp_1'=8,'fsdp_2'=2,'dp'=8] {'dp'}, use_global_device_ids=true, to_apply=%region_4.5 | all-reduce | flops 1 | bytes 8 | tf_op jit(solution)/shard_map/psum | solution.py:98
  138.9 0.7 fusion.5
  139.6 0.0 all-gather.5.cloned.1.call-update
  139.6 37.9 %all-gather.5.cloned.1.call-done = bf16[1024,1,1024]{2,0,1:T(8,128)(2,1)} async-done(((bf16[128,1,1024]{2,0,1:T(8,128)(2,1)}), bf16[1024,1,1024]{2,0,1:T(8,128)(2,1)}) %all-gather.5.cloned.1.call-update) | async-done | bytes 2097168 | tf_op jit(solution)/shard_map/all_gather | solution.py:101
  177.6 1.8 copy.88
  179.3 5.4 %all_to_all.34 = bf16[32,2,16,1,1024]{4,2,0,3,1:T(8,128)(2,1)S(1)} all-to-all(bf16[32,2,16,1,1024]{4,2,0,3,1:T(8,128)(2,1)S(1)} %copy.88), channel_id=1, replica_groups=mesh['fsdp_0'=4,'fsdp_1'=8,'fsdp_2'=2,'dp'=8] {'fsdp_2'}, dimensions={1} | all-to-all | bytes 4194304 | tf_op jit(solution)/shard_map/all_to_all | solution.py:39
  184.8 1.5 copy.89
  186.2 0.0 copy-start.1
  186.2 10.0 %all-to-all-start.3 = ((bf16[32,2,16,1,1024]{4,2,1,3,0:T(8,128)(2,1)}), bf16[32,2,16,1,1024]{4,2,1,3,0:T(8,128)(2,1)}, u32[]{:S(2)}, u32[]{:S(2)}) async-start(bf16[32,2,16,1,1024]{4,2,1,3,0:T(8,128)(2,1)} %copy.89), calls=%async_computation.3 | async-start | bytes 4194304 | tf_op jit(solution)/shard_map/all_to_all | solution.py:39
  196.2 0.0 copy-start.2
  196.3 0.1 broadcast_in_dim.62
  196.4 0.1 broadcast_in_dim.63
  196.4 0.0 copy-done.1
  196.5 1.6 fusion.3
  198.1 0.0 copy-done.2
  198.1 1.3 fusion.2
  199.4 47.3 %all-to-all-done.3 = bf16[32,2,16,1,1024]{4,2,1,3,0:T(8,128)(2,1)} async-done(((bf16[32,2,16,1,1024]{4,2,1,3,0:T(8,128)(2,1)}), bf16[32,2,16,1,1024]{4,2,1,3,0:T(8,128)(2,1)}, u32[]{:S(2)}, u32[]{:S(2)}) %all-to-all-start.3) | async-done | bytes 2097184 | tf_op jit(solution)/shard_map/all_to_all | solution.py:39
  246.6 2.2 gather_fusion.2
  248.8 0.1 copy.92
  248.9 1.1 broadcast_select_fusion
  (13 shorter events, 0.2 us)
Async XLA Ops:
  7.2 110.4 %copy-start = (bf16[1,128,1024]{2,1,0:T(8,128)(2,1)S(1)}, bf16[1,128,1024]{2,1,0:T(8,128)(2,1)}, u32[]{:S(2)}) copy-start(bf16[1,128,1024]{2,1,0:T(8,128)(2,1)} %param.10) | copy-start | bytes 786436
  8.5 12.4 %copy-start.4 = (s32[28]{0:T(128)S(1)}, s32[28]{0:T(128)}, u32[]{:S(2)}) copy-start(s32[28]{0:T(128)} %param.7) | copy-start | bytes 340
  9.8 35.7 %all-to-all-start = ((bf16[8,16,28,128]{3,1,2,0:T(8,128)(2,1)}), bf16[8,16,28,128]{3,1,2,0:T(8,128)(2,1)S(1)}, u32[]{:S(2)}, u32[]{:S(2)}) async-start(bf16[8,16,28,128]{3,1,2,0:T(8,128)(2,1)} %copy.74), calls=%async_computation | async-start | bytes 1835008 | tf_op jit(solution)/shard_map/all_to_all | solution.py:25
  20.1 97.4 %all-gather.3.cloned.1.call-start = ((), (), s32[]{:S(2)}) async-start(), calls=%async_computation.4 | async-start | bytes 2359296 | tf_op jit(solution)/shard_map/all_gather | solution.py:84
  20.9 156.7 %all-gather.5.cloned.1.call-start = ((), (), s32[]{:S(2)}) async-start(), calls=%async_computation.5 | async-start | bytes 2359296 | tf_op jit(solution)/shard_map/all_gather | solution.py:101
  68.1 11.4 %collective-permute-start = (bf16[1024,1,128]{2,0,1:T(8,128)(2,1)S(1)}, bf16[1024,1,128]{2,0,1:T(8,128)(2,1)S(1)}, u32[]{:S(2)}, u32[]{:S(2)}) collective-permute-start(bf16[1024,1,128]{2,0,1:T(8,128)(2,1)S(1)} %bitcast.123), channel_id=1, source_target_pairs={{0,1},{1,2},{2,3},{3,4},{4,5},{5,6},{6,7},{7,0},{8,9},{9,10},{10,1... | collective-permute-start | bytes 786440 | tf_op jit(solution)/shard_map/ppermute | solution.py:76
  79.5 10.6 %collective-permute-start.1 = (bf16[1024,1,128]{2,0,1:T(8,128)(2,1)S(1)}, bf16[1024,1,128]{2,0,1:T(8,128)(2,1)S(1)}, u32[]{:S(2)}, u32[]{:S(2)}) collective-permute-start(bf16[1024,1,128]{2,0,1:T(8,128)(2,1)S(1)} %collective-permute-done), channel_id=1, source_target_pairs={{0,1},{1,2},{2,3},{3,4},{4,5},{5,6},{6,7},{7,0},{8,9},{9,10},{10,1... | collective-permute-start | bytes 786440 | tf_op jit(solution)/shard_map/ppermute | solution.py:76
  83.8 9.4 %collective-permute-start.4 = (bf16[1024,1,128]{2,0,1:T(8,128)(2,1)S(1)}, bf16[1024,1,128]{2,0,1:T(8,128)(2,1)S(1)}, u32[]{:S(2)}, u32[]{:S(2)}) collective-permute-start(bf16[1024,1,128]{2,0,1:T(8,128)(2,1)S(1)} %bitcast.124), channel_id=1, source_target_pairs={{1,0},{2,1},{3,2},{4,3},{5,4},{6,5},{7,6},{0,7},{9,8},{10,9},{11,1... | collective-permute-start | bytes 786440 | tf_op jit(solution)/shard_map/ppermute | solution.py:78
  90.1 9.7 %collective-permute-start.2 = (bf16[1024,1,128]{2,0,1:T(8,128)(2,1)S(1)}, bf16[1024,1,128]{2,0,1:T(8,128)(2,1)S(1)}, u32[]{:S(2)}, u32[]{:S(2)}) collective-permute-start(bf16[1024,1,128]{2,0,1:T(8,128)(2,1)S(1)} %collective-permute-done.1), channel_id=1, source_target_pairs={{0,1},{1,2},{2,3},{3,4},{4,5},{5,6},{6,7},{7,0},{8,9},{9,10},{10,1... | collective-permute-start | bytes 786440 | tf_op jit(solution)/shard_map/ppermute | solution.py:76
  93.1 8.6 %collective-permute-start.5 = (bf16[1024,1,128]{2,0,1:T(8,128)(2,1)S(1)}, bf16[1024,1,128]{2,0,1:T(8,128)(2,1)}, u32[]{:S(2)}, u32[]{:S(2)}) collective-permute-start(bf16[1024,1,128]{2,0,1:T(8,128)(2,1)S(1)} %collective-permute-done.4), channel_id=1, source_target_pairs={{1,0},{2,1},{3,2},{4,3},{5,4},{6,5},{7,6},{0,7},{9,8},{10,9},{11,1... | collective-permute-start | bytes 786440 | tf_op jit(solution)/shard_map/ppermute | solution.py:78
  99.8 7.1 %copy-start.3 = (bf16[1024,1,128]{2,0,1:T(8,128)(2,1)}, bf16[1024,1,128]{2,0,1:T(8,128)(2,1)S(1)}, u32[]{:S(2)}) copy-start(bf16[1024,1,128]{2,0,1:T(8,128)(2,1)S(1)} %collective-permute-done.2) | copy-start | bytes 786436
  99.8 9.6 %collective-permute-start.3 = (bf16[1024,1,128]{2,0,1:T(8,128)(2,1)S(1)}, bf16[1024,1,128]{2,0,1:T(8,128)(2,1)}, u32[]{:S(2)}, u32[]{:S(2)}) collective-permute-start(bf16[1024,1,128]{2,0,1:T(8,128)(2,1)S(1)} %collective-permute-done.2), channel_id=1, source_target_pairs={{0,1},{1,2},{2,3},{3,4},{4,5},{5,6},{6,7},{7,0},{8,9},{9,10},{10,1... | collective-permute-start | bytes 786440 | tf_op jit(solution)/shard_map/ppermute | solution.py:76
  101.8 10.7 %collective-permute-start.6 = (bf16[1024,1,128]{2,0,1:T(8,128)(2,1)}, bf16[1024,1,128]{2,0,1:T(8,128)(2,1)S(1)}, u32[]{:S(2)}, u32[]{:S(2)}) collective-permute-start(bf16[1024,1,128]{2,0,1:T(8,128)(2,1)} %collective-permute-done.5), channel_id=1, source_target_pairs={{1,0},{2,1},{3,2},{4,3},{5,4},{6,5},{7,6},{0,7},{9,8},{10,9},{11,1... | collective-permute-start | bytes 786440 | tf_op jit(solution)/shard_map/ppermute | solution.py:78
  186.2 10.2 %copy-start.1 = (f32[1,128,1024]{2,1,0:T(8,128)S(1)}, f32[1,128,1024]{2,1,0:T(8,128)}, u32[]{:S(2)}) copy-start(f32[1,128,1024]{2,1,0:T(8,128)} %param.9) | copy-start | bytes 1572868
  186.2 60.4 %all-to-all-start.3 = ((bf16[32,2,16,1,1024]{4,2,1,3,0:T(8,128)(2,1)}), bf16[32,2,16,1,1024]{4,2,1,3,0:T(8,128)(2,1)}, u32[]{:S(2)}, u32[]{:S(2)}) async-start(bf16[32,2,16,1,1024]{4,2,1,3,0:T(8,128)(2,1)} %copy.89), calls=%async_computation.3 | async-start | bytes 4194304 | tf_op jit(solution)/shard_map/all_to_all | solution.py:39
  196.2 1.8 copy-start.2
Sparse Core Ops, SparseCore 0:
  23.0 47.5 all-gather.2
  139.7 37.7 all-gather.4
